TPU v7x, 32 devices: a whole 2x2x4 slice. The times are simulated.
32 devices in a mesh: space: 8 (over z, y), level: 4 (over x, core).
Axes of the slice: x: 2, y: 2, z: 4, core: 2. Of those that a mesh axis runs over, the one named last changes fastest.
Arguments:
- grid_latent: bfloat16 [4096, 512], P('space'), may hold values from -6 to 6
- mesh_latent: bfloat16 [4, 64, 512], P('level', 'space'), may hold values from -6 to 6
- grid_output_cotangent: bfloat16 [4096, 512], P('space'), may hold values from -6 to 6
- w_send: bfloat16 [512, 512], replicated, may hold values from -0.25 to 0.25
- w_recv: bfloat16 [512, 512], replicated, may hold values from -0.25 to 0.25
- output_weight: bfloat16 [512, 512], replicated, may hold values from -0.25 to 0.25
- hidden_layer_bias: float32 [512], replicated, may hold values from -4 to 4
- output_norm_gain: float32 [512], replicated, may hold values from 0.1 to 1.9
- edge_sender: int32 [4, 16384], P('level', 'space'), may hold values from 0 to 23
- edge_receiver: int32 [4, 16384], P('level', 'space'), may hold values from 0 to 511
- edge_live: int32 [4, 16384], P('level', 'space'), may hold values 0 or 1
Outputs:
- d_grid: float32 [4096, 512], P(('space', 'level'))
- d_mesh: float32 [4, 64, 512], P('level', 'space')
- d_w_send: bfloat16 [512, 512], replicated
- d_w_recv: bfloat16 [512, 512], replicated
- d_w_out: bfloat16 [512, 512], replicated
- d_bias: float32 [512], replicated
- d_gain: float32 [512], replicated
All inputs are finite; a program needn't handle non-finite values. No bound on the sum of `edge_live` on one device may be relied on, other than what follows from the above.
Results may differ from a plain program's by a relative error of at most 0.012.
Values may be sent and summed in bfloat16 or wider, within the bound.
No kernel may reach another device: no remote copies, remote signals or barrier semaphores. Data moves between devices by JAX's collectives and lax.ppermute only.
A program may use at most 64 MiB of HBM per device.

v0:
```python
import jax
import jax.numpy as jnp
from jax import lax
from jax.sharding import PartitionSpec as P


def with_halo(cells, sides, width):
    for axis, dim in sides:
        count = lax.axis_size(axis)
        ends = count - 1
        head = lax.slice_in_dim(cells, 0, width, axis=dim)
        tail = lax.slice_in_dim(cells, cells.shape[dim] - width, cells.shape[dim], axis=dim)
        cells = jnp.concatenate(
            [
                lax.ppermute(tail, axis, [(i, (i + 1) % count) for i in range(ends)]),
                cells,
                lax.ppermute(head, axis, [((i + 1) % count, i) for i in range(ends)]),
            ],
            axis=dim,
        )
    return cells


def from_behind(block, axis, distance):
    devices = range(lax.axis_size(axis))
    route = [(i - distance, i) for i in devices if i - distance in devices]
    return lax.ppermute(block, axis, route)


def edge_reverse_step(
    sending_rows,
    receiver_rows,
    cotangent_lines,
    slot_active_flags,
    output_weight,
    hidden_layer_bias,
    output_norm_gain,
):
    preact = sending_rows + receiver_rows + hidden_layer_bias
    hidden = jax.nn.silu(preact).astype(jnp.bfloat16)
    outer = jnp.dot(hidden, output_weight, preferred_element_type=jnp.float32)
    center = outer - jnp.mean(outer, axis=-1, keepdims=True)
    inv_scale = lax.rsqrt(jnp.mean(center * center, axis=-1, keepdims=True) + 1e-05)
    normed = center * inv_scale
    incoming_gradient = cotangent_lines.astype(jnp.float32) * slot_active_flags[:, None].astype(
        jnp.float32
    )
    scaled = incoming_gradient * output_norm_gain
    d_outer = inv_scale * (
        scaled
        - jnp.mean(scaled, axis=-1, keepdims=True)
        - normed * jnp.mean(scaled * normed, axis=-1, keepdims=True)
    )
    d_outer_b = d_outer.astype(jnp.bfloat16)
    w_out_grad = jnp.dot(hidden.T, d_outer_b, preferred_element_type=jnp.float32)
    d_hidden = jnp.dot(d_outer_b, output_weight.T, preferred_element_type=jnp.float32)
    sigmoid = jax.nn.sigmoid(preact)
    preactivation_gradient = d_hidden * sigmoid * (1.0 + preact * (1.0 - sigmoid))
    return (
        preactivation_gradient,
        w_out_grad,
        jnp.sum(preactivation_gradient, axis=0),
        jnp.sum(incoming_gradient * normed, axis=0),
    )


def body(
    grid_latent,
    mesh_latent,
    grid_output_cotangent,
    w_send,
    w_recv,
    output_weight,
    hidden_layer_bias,
    output_norm_gain,
    edge_sender,
    edge_receiver,
    edge_live,
):
    shards = lax.axis_size("space")
    width = grid_latent.shape[1]
    grid_rows = grid_latent.shape[0]
    mesh_rows = mesh_latent.shape[1]
    slots = edge_sender.shape[1]
    sender_local = edge_sender[0]
    receiver_index = edge_receiver[0]
    band = lax.axis_index("space")
    window = sender_local // mesh_rows
    target = band + window - 1
    inside = (target >= 0) & (target < shards)
    window = jnp.where(inside, window, 1)
    table_row = window * mesh_rows + sender_local % mesh_rows
    proj_send = jnp.dot(mesh_latent[0], w_send, preferred_element_type=jnp.float32).astype(
        jnp.bfloat16
    )
    projected_receiver = jnp.dot(grid_latent, w_recv, preferred_element_type=jnp.float32)
    table = with_halo(proj_send, (("space", 0),), mesh_rows)
    sending_rows = table[table_row]
    block = 512
    blocks = slots // block

    def run_block(operands):
        rows_send, rows_recv, rows_cot, rows_live = operands
        return edge_reverse_step(
            rows_send.astype(jnp.float32),
            rows_recv,
            rows_cot,
            rows_live,
            output_weight,
            hidden_layer_bias,
            output_norm_gain,
        )

    operands = (
        sending_rows.reshape(blocks, block, width),
        projected_receiver[receiver_index].reshape(blocks, block, width),
        grid_output_cotangent[receiver_index].reshape(blocks, block, width),
        edge_live[0].reshape(blocks, block),
    )
    d_pre_blocks, wout_blocks, bias_blocks, gain_blocks = lax.map(run_block, operands)
    preactivation_gradient = d_pre_blocks.reshape(slots, width)
    output_weight_piece = jnp.sum(wout_blocks, axis=0)
    bias_piece = jnp.sum(bias_blocks, axis=0)
    gain_piece = jnp.sum(gain_blocks, axis=0)
    table_grads = jax.ops.segment_sum(preactivation_gradient, table_row, num_segments=3 * mesh_rows)
    below = table_grads[:mesh_rows]
    above = table_grads[2 * mesh_rows :]
    from_below = from_behind(above, "space", 1)
    from_above = from_behind(below, "space", -1)
    mesh_acc = table_grads[mesh_rows : 2 * mesh_rows] + from_below + from_above
    grid_local = jax.ops.segment_sum(preactivation_gradient, receiver_index, num_segments=grid_rows)
    share = grid_rows // lax.axis_size("level")
    offset = lax.axis_index("level") * share
    grid_acc = lax.psum_scatter(
        grid_local.astype(jnp.bfloat16), "level", scatter_dimension=0, tiled=True
    )
    grid_part = lax.dynamic_slice_in_dim(grid_latent, offset, share, 0)
    mesh_sum = mesh_acc.astype(jnp.bfloat16)
    d_mesh = jnp.dot(mesh_sum, w_send.T, preferred_element_type=jnp.float32)[None]
    d_grid = jnp.dot(grid_acc, w_recv.T, preferred_element_type=jnp.float32)
    wsend_part = jnp.dot(mesh_latent[0].T, mesh_sum, preferred_element_type=jnp.float32)
    wrecv_part = jnp.dot(grid_part.T, grid_acc, preferred_element_type=jnp.float32)
    totals = lax.psum(
        (wsend_part, wrecv_part, output_weight_piece, bias_piece, gain_piece), ("space", "level")
    )
    d_w_send = totals[0].astype(jnp.bfloat16)
    d_w_recv = totals[1].astype(jnp.bfloat16)
    d_w_out = totals[2].astype(jnp.bfloat16)
    d_bias = totals[3]
    d_gain = totals[4]
    return (d_grid, d_mesh, d_w_send, d_w_recv, d_w_out, d_bias, d_gain)


def solution(mesh):
    return jax.shard_map(
        body,
        mesh=mesh,
        in_specs=(
            P("space", None),
            P("level", "space", None),
            P("space", None),
            P(),
            P(),
            P(),
            P(),
            P(),
            P("level", "space"),
            P("level", "space"),
            P("level", "space"),
        ),
        out_specs=(P(("space", "level"), None), P("level", "space", None), P(), P(), P(), P(), P()),
        check_vma=False,
    )
```

profile of v0, /device:TPU:0, one launch (start us, length us, event | category | flops | bytes accessed | tf_op | source)
XLA Modules:
  0.0 218.6 jit_solution(9644242598406611209)
XLA Ops:
  7.2 1.3 convolution_convert_fusion
  8.5 1.3 collective-permute-start.1
  9.8 5.5 %collective-permute-start = (bf16[8,512]{1,0:T(8,128)(2,1)S(1)}, bf16[8,512]{1,0:T(8,128)(2,1)S(1)}, u32[]{:S(2)}, u32[]{:S(2)}) collective-permute-start(bf16[8,512]{1,0:T(8,128)(2,1)S(1)} %convolution_convert_fusion), channel_id=1, source_target_pairs={{0,4},{4,8},{8,12},{12,16},{16,20},{20,24},{24,28},{1,5},{5,9},{9,... | collective-permute-start | bytes 24584 | tf_op jit(solution)/shard_map/ppermute | solution.py:15
  15.3 0.7 compare_select_fusion
  16.1 0.8 compare_select_fusion.1
  16.9 1.6 fusion.27
  18.5 0.5 broadcast.290
  19.1 1.4 reduce.3
  20.5 9.2 %gather_fusion.2 = bf16[2048,512]{1,0:T(8,128)(2,1)} fusion(bf16[512,512]{1,0:T(8,128)(2,1)S(1)} %copy-done, s32[2048]{0:T(1024)S(1)} %broadcast_clamp_fusion), kind=kCustom, calls=%fused_computation.2 | custom fusion | bytes 4202496 | tf_op jit(solution)/shard_map/gather | solution.py:117
  29.6 8.9 %gather_fusion.1 = f32[2048,512]{1,0:T(8,128)} fusion(f32[512,512]{1,0:T(8,128)S(1)} %fusion.27, s32[2048]{0:T(1024)S(1)} %broadcast_clamp_fusion), kind=kCustom, calls=%fused_computation.1 | custom fusion | bytes 8396800 | tf_op jit(solution)/shard_map/gather | solution.py:116
  38.6 9.2 %gather_fusion = bf16[2048,512]{1,0:T(8,128)(2,1)} fusion(bf16[24,512]{1,0:T(8,128)(2,1)S(1)} %pad_maximum_fusion, s32[2048]{0:T(1024)S(1)} %broadcast_clamp_fusion.1), kind=kCustom, calls=%fused_computation | custom fusion | bytes 4202496 | tf_op jit(solution)/shard_map/gather | solution.py:98
  47.8 37.2 %while.16 = (s32[]{:T(128)}, f32[4,512,512]{2,1,0:T(8,128)}, f32[4,512,512]{2,1,0:T(8,128)}, f32[4,512]{1,0:T(4,128)S(1)}, f32[4,512]{1,0:T(4,128)S(1)}, /*index...) while((s32[]{:T(128)}, f32[4,512,512]{2,1,0:T(8,128)}, ...), condition=%wide.region_7.8_spmd, body=%wide.region_0.7_spmd.sunk | while | flops 816840704 | bytes 18942132 | solution.py:120
  47.8 1.7 multiply_convert_fusion.2
  49.5 1.1 constant_dynamic-slice_fusion.2
  50.8 0.5 fusion.60
  51.5 0.5 fusion.61
  51.9 0.3 fusion.62
  52.3 1.6 fusion.63
  53.9 3.0 %bitcast_dynamic-update-slice_fusion.2 = (f32[4,512,512]{2,1,0:T(8,128)}, f32[512,512]{1,0:T(8,128)S(1)}) fusion(f32[4,512,512]{2,1,0:T(8,128)} %get-tuple-element.263, s32[]{:T(128)S(6)} %copy.34, f32[512]{0:T(512)S(1)} %get-tuple-element.284, f32[4,512,512]{2,1,0:T(8,128)} %get-tuple-element.283, bf16[4,512,512]{2,1,0:T(8,128)(2,1)} %get-tuple-element.282, ...), kind=kOutput, calls=%fused_computation.20.clone.1 | convolution fusion | flops 271319040 | bytes 4720644 | tf_op jit(solution)/shard_map/while/body/eval_jaxpr/dot_general | solution.py:56
  57.1 1.7 multiply_convert_fusion.2
  58.8 1.1 constant_dynamic-slice_fusion.2
  60.1 0.5 fusion.60
  60.8 0.5 fusion.61
  61.7 1.5 fusion.63
  63.2 3.1 %bitcast_dynamic-update-slice_fusion.2 = (f32[4,512,512]{2,1,0:T(8,128)}, f32[512,512]{1,0:T(8,128)S(1)}) fusion(f32[4,512,512]{2,1,0:T(8,128)} %get-tuple-element.263, s32[]{:T(128)S(6)} %copy.34, f32[512]{0:T(512)S(1)} %get-tuple-element.284, f32[4,512,512]{2,1,0:T(8,128)} %get-tuple-element.283, bf16[4,512,512]{2,1,0:T(8,128)(2,1)} %get-tuple-element.282, ...), kind=kOutput, calls=%fused_computation.20.clone.1 | convolution fusion | flops 271319040 | bytes 4720644 | tf_op jit(solution)/shard_map/while/body/eval_jaxpr/dot_general | solution.py:56
  66.4 1.7 multiply_convert_fusion.2
  68.1 1.1 constant_dynamic-slice_fusion.2
  69.4 0.5 fusion.60
  70.1 0.5 fusion.61
  71.0 1.5 fusion.63
  72.5 3.1 %bitcast_dynamic-update-slice_fusion.2 = (f32[4,512,512]{2,1,0:T(8,128)}, f32[512,512]{1,0:T(8,128)S(1)}) fusion(f32[4,512,512]{2,1,0:T(8,128)} %get-tuple-element.263, s32[]{:T(128)S(6)} %copy.34, f32[512]{0:T(512)S(1)} %get-tuple-element.284, f32[4,512,512]{2,1,0:T(8,128)} %get-tuple-element.283, bf16[4,512,512]{2,1,0:T(8,128)(2,1)} %get-tuple-element.282, ...), kind=kOutput, calls=%fused_computation.20.clone.1 | convolution fusion | flops 271319040 | bytes 4720644 | tf_op jit(solution)/shard_map/while/body/eval_jaxpr/dot_general | solution.py:56
  75.7 1.7 multiply_convert_fusion.2
  77.4 1.1 constant_dynamic-slice_fusion.2
  78.7 0.5 fusion.60
  79.4 0.5 fusion.61
  80.3 1.5 fusion.63
  81.7 3.0 %bitcast_dynamic-update-slice_fusion.2 = (f32[4,512,512]{2,1,0:T(8,128)}, f32[512,512]{1,0:T(8,128)S(1)}) fusion(f32[4,512,512]{2,1,0:T(8,128)} %get-tuple-element.263, s32[]{:T(128)S(6)} %copy.34, f32[512]{0:T(512)S(1)} %get-tuple-element.284, f32[4,512,512]{2,1,0:T(8,128)} %get-tuple-element.283, bf16[4,512,512]{2,1,0:T(8,128)(2,1)} %get-tuple-element.282, ...), kind=kOutput, calls=%fused_computation.20.clone.1 | convolution fusion | flops 271319040 | bytes 4720644 | tf_op jit(solution)/shard_map/while/body/eval_jaxpr/dot_general | solution.py:56
  84.9 13.5 %scatter_custom_fusion = f32[512,512]{1,0:T(8,128)S(1)} fusion(s32[2048]{0:T(1024)} %bitcast.107, f32[2048,512]{1,0:T(8,128)} %bitcast.108, f32[]{:T(128)} %constant.75.clone.1), kind=kCustom, calls=%fused_computation.35 | custom fusion | flops 1048576 | bytes 1049088 | tf_op jit(solution)/shard_map/scatter-add | solution.py:131
  98.4 0.9 convert_element_type.46
  99.3 13.2 %scatter_custom_fusion.1 = f32[24,512]{1,0:T(8,128)S(1)} fusion(s32[2048]{0:T(1024)S(1)} %bitcast.106, f32[2048,512]{1,0:T(8,128)} %bitcast.109, f32[]{:T(128)} %constant.75.clone.1), kind=kCustom, calls=%fused_computation.45 | custom fusion | flops 1048576 | bytes 49664 | tf_op jit(solution)/shard_map/scatter-add | solution.py:125
  112.6 4.8 %collective-permute-start.2 = (f32[8,512]{1,0:T(8,128)S(1)}, f32[8,512]{1,0:T(8,128)S(1)}, u32[]{:S(2)}, u32[]{:S(2)}) collective-permute-start(f32[8,512]{1,0:T(8,128)S(1)} %get-tuple-element.154), channel_id=1, source_target_pairs={{0,4},{4,8},{8,12},{12,16},{16,20},{20,24},{24,28},{1,5},{5,9},{9,... | collective-permute-start | bytes 49160 | tf_op jit(solution)/shard_map/ppermute | solution.py:27
  117.4 1.5 collective-permute-start.3
  118.9 3.8 %reduce_sum.81 = f32[512,512]{1,0:T(8,128)} reduce(f32[4,512,512]{2,1,0:T(8,128)} %get-tuple-element.73, f32[]{:T(128)} %constant.75.clone.1), dimensions={0}, to_apply=%region_13.14 | reduce | flops 786432 | bytes 5242884 | tf_op jit(solution)/shard_map/reduce_sum | solution.py:122
  123.4 0.9 convolution_bitcast_fusion.2
  124.3 1.3 fusion.14
  125.6 83.1 %all-reduce.2 = (bf16[512,512]{0,1:T(8,128)(2,1)}, bf16[512,512]{1,0:T(8,128)(2,1)}, bf16[512,512]{1,0:T(8,128)(2,1)}, f32[512]{0:T(512)}, f32[512]{0:T(512)}) all-reduce(f32[512,512]{0,1:T(8,128)S(1)} %convolution_bitcast_fusion.1, f32[512,512]{1,0:T(8,128)S(1)} %fusion.14, ...), channel_id=1, replica_groups=mesh['space'=8,'level'=4] {'space','level'}, use_global_device_ids=true, to_apply=%region_11.12 | all-reduce | flops 787456 | bytes 4726784 | tf_op jit(solution)/shard_map/psum | solution.py:143
  208.7 2.0 copy.21
  210.7 1.0 fusion.28
  (75 shorter events, 4.4 us)
Async XLA Ops:
  7.2 13.3 %copy-start = (bf16[512,512]{1,0:T(8,128)(2,1)S(1)}, bf16[512,512]{1,0:T(8,128)(2,1)}, u32[]{:S(2)}) copy-start(bf16[512,512]{1,0:T(8,128)(2,1)} %param.15) | copy-start | bytes 1572868
  7.2 117.1 %reduce-scatter.2.cloned.1.call-start = ((), (), s32[]{:S(2)}) async-start(), calls=%async_computation.1 | async-start | bytes 655360 | tf_op jit(solution)/shard_map/reduce_scatter | solution.py:134
  8.5 30.0 %collective-permute-start.1 = (bf16[8,512]{1,0:T(8,128)(2,1)S(1)}, bf16[8,512]{1,0:T(8,128)(2,1)S(1)}, u32[]{:S(2)}, u32[]{:S(2)}) collective-permute-start(bf16[8,512]{1,0:T(8,128)(2,1)S(1)} %convolution_convert_fusion), channel_id=1, source_target_pairs={{4,0},{8,4},{12,8},{16,12},{20,16},{24,20},{28,24},{5,1},{9,5},{13... | collective-permute-start | bytes 24584 | tf_op jit(solution)/shard_map/ppermute | solution.py:17
  9.8 28.7 %collective-permute-start = (bf16[8,512]{1,0:T(8,128)(2,1)S(1)}, bf16[8,512]{1,0:T(8,128)(2,1)S(1)}, u32[]{:S(2)}, u32[]{:S(2)}) collective-permute-start(bf16[8,512]{1,0:T(8,128)(2,1)S(1)} %convolution_convert_fusion), channel_id=1, source_target_pairs={{0,4},{4,8},{8,12},{12,16},{16,20},{20,24},{24,28},{1,5},{5,9},{9,... | collective-permute-start | bytes 24584 | tf_op jit(solution)/shard_map/ppermute | solution.py:15
  38.5 9.2 %copy-start.1 = (bf16[512,512]{1,0:T(8,128)(2,1)S(1)}, bf16[512,512]{1,0:T(8,128)(2,1)}, u32[]{:S(2)}) copy-start(bf16[512,512]{1,0:T(8,128)(2,1)} %param.18) | copy-start | bytes 1572868
  38.5 9.2 %copy-start.5 = (f32[512]{0:T(512)S(1)}, f32[512]{0:T(512)}, u32[]{:S(2)}) copy-start(f32[512]{0:T(512)} %param.20) | copy-start | bytes 6148
  38.5 9.2 %copy-start.6 = (f32[512]{0:T(512)S(1)}, f32[512]{0:T(512)}, u32[]{:S(2)}) copy-start(f32[512]{0:T(512)} %param.19) | copy-start | bytes 6148
  84.9 38.1 %copy-start.7 = (bf16[1,8,512]{2,1,0:T(8,128)(2,1)S(1)}, bf16[1,8,512]{2,1,0:T(8,128)(2,1)}, u32[]{:S(2)}) copy-start(bf16[1,8,512]{2,1,0:T(8,128)(2,1)} %param.14) | copy-start | bytes 24580
  98.4 25.0 %copy-start.2 = (bf16[512,512]{1,0:T(8,128)(2,1)S(1)}, bf16[512,512]{1,0:T(8,128)(2,1)}, u32[]{:S(2)}) copy-start(bf16[512,512]{1,0:T(8,128)(2,1)} %param.16) | copy-start | bytes 1572868
  112.6 10.1 %collective-permute-start.2 = (f32[8,512]{1,0:T(8,128)S(1)}, f32[8,512]{1,0:T(8,128)S(1)}, u32[]{:S(2)}, u32[]{:S(2)}) collective-permute-start(f32[8,512]{1,0:T(8,128)S(1)} %get-tuple-element.154), channel_id=1, source_target_pairs={{0,4},{4,8},{8,12},{12,16},{16,20},{20,24},{24,28},{1,5},{5,9},{9,... | collective-permute-start | bytes 49160 | tf_op jit(solution)/shard_map/ppermute | solution.py:27
  117.4 5.6 %collective-permute-start.3 = (f32[8,512]{1,0:T(8,128)S(1)}, f32[8,512]{1,0:T(8,128)S(1)}, u32[]{:S(2)}, u32[]{:S(2)}) collective-permute-start(f32[8,512]{1,0:T(8,128)S(1)} %get-tuple-element.155), channel_id=1, source_target_pairs={{4,0},{8,4},{12,8},{16,12},{20,16},{24,20},{28,24},{5,1},{9,5},{13... | collective-permute-start | bytes 49160 | tf_op jit(solution)/shard_map/ppermute | solution.py:27
  122.7 88.0 %copy-start.3 = (bf16[512,512]{1,0:T(8,128)(2,1)S(1)}, bf16[512,512]{1,0:T(8,128)(2,1)}, u32[]{:S(2)}) copy-start(bf16[512,512]{1,0:T(8,128)(2,1)} %param.17) | copy-start | bytes 1572868
  124.3 86.5 %copy-start.4 = (bf16[128,512]{1,0:T(8,128)(2,1)S(1)}, bf16[128,512]{1,0:T(8,128)(2,1)}, u32[]{:S(2)}) copy-start(bf16[128,512]{1,0:T(8,128)(2,1)} %reduce-scatter.2.cloned.1.call-done) | copy-start | bytes 393220
Sparse Core Ops, SparseCore 0:
  99.4 23.2 reduce-scatter.1
where the time goes:
time: 220 us; the launch traced here: 219 us
  blocking collectives  83.1 us (38%)
  other arithmetic  45.5 us (21%)
  local copies, waits for them, and re-layouts  35.4 us (16%)
  matrix products  26.6 us (12%)
  between operations  14.3 us (6%)
  starting transfers between devices  13.2 us (6%)
    psum x1, blocking collectives, body(): lax.psum((wsend_part, wrecv_part, output_weight_piece, bias_piece, gain_p...  83.1 us
    scatter-add x1, other arithmetic, body(): jax.ops.segment_sum(preactivation_gradient, receiver_index, num_segments=...  13.5 us
    scatter-add x1, other arithmetic, body(): jax.ops.segment_sum(preactivation_gradient, table_row, num_segments=3 * m...  13.2 us
    dot_general x4, matrix products, edge_reverse_step(): jnp.dot(d_outer_b, output_weight.T, preferred_element_type=jnp.float32)  12.2 us
    gather x1, local copies, waits for them, and re-layouts, body(): sending_rows = table[table_row]  9.18 us
    gather x1, local copies, waits for them, and re-layouts, body(): grid_output_cotangent[receiver_index].reshape(blocks, block, width)  9.15 us
    gather x1, local copies, waits for them, and re-layouts, body(): projected_receiver[receiver_index].reshape(blocks, block, width)  8.9 us
    convert_element_type x4, other arithmetic, edge_reverse_step(): hidden = jax.nn.silu(preact).astype(jnp.bfloat16)  6.68 us
  transfers between devices with their start and end apart: 5, of which 1 were waited for; matrix products, arithmetic and copies ran while one was open for 19% of the time, Pallas kernels for 0%

commit v1 on v0

--- a/solution.py
+++ b/solution.py
@@ -141,7 +141,8 @@
     wsend_part = jnp.dot(mesh_latent[0].T, mesh_sum, preferred_element_type=jnp.float32)
     wrecv_part = jnp.dot(grid_part.T, grid_acc, preferred_element_type=jnp.float32)
     totals = lax.psum(
-        (wsend_part, wrecv_part, output_weight_piece, bias_piece, gain_piece), ("space", "level")
+        lax.psum((wsend_part, wrecv_part, output_weight_piece, bias_piece, gain_piece), "space"),
+        "level",
     )
     d_w_send = totals[0].astype(jnp.bfloat16)
     d_w_recv = totals[1].astype(jnp.bfloat16)

time: 220 us -> 326 us (1.48)
  waiting for transfers between devices: 0.36 us -> 108 us
    psum x0 -> x1, waiting for transfers between devices: none -> 108 us  [body(): lax.psum((wsend_part, wrecv_part, output_weight_piece, bias_piece, gain_p...]
    psum x1, blocking collectives: 83.1 us -> 20.9 us  [body(): lax.psum((wsend_part, wrecv_part, output_weight_piece, bias_piece, gain_p...]
    psum x0 -> x1, blocking collectives: none -> 59.8 us  [body(): lax.psum(lax.psum((wsend_part, wrecv_part, output_weight_piece, bias_piec...]
  transfers between devices with their start and end apart: 5 -> 6, of which waited for: 1 -> 2; matrix products, arithmetic and copies ran while one was open for 19% -> 13% of each run, Pallas kernels for 0% -> 0%
where the time goes in v1:
time: 326 us; the launch traced here: 325 us
  waiting for transfers between devices  108 us (33%)
  blocking collectives  80.7 us (25%)
  other arithmetic  45.5 us (14%)
  local copies, waits for them, and re-layouts  34.4 us (11%)
  matrix products  28.6 us (9%)
  between operations  14.3 us (4%)
  starting transfers between devices  13.2 us (4%)
    psum x1, waiting for transfers between devices, body(): lax.psum((wsend_part, wrecv_part, output_weight_piece, bias_piece, gain_p...  108 us
    psum x1, blocking collectives, body(): lax.psum(lax.psum((wsend_part, wrecv_part, output_weight_piece, bias_piec...  59.8 us
    psum x1, blocking collectives, body(): lax.psum((wsend_part, wrecv_part, output_weight_piece, bias_piece, gain_p...  20.9 us
    scatter-add x1, other arithmetic, body(): jax.ops.segment_sum(preactivation_gradient, receiver_index, num_segments=...  13.5 us
    scatter-add x1, other arithmetic, body(): jax.ops.segment_sum(preactivation_gradient, table_row, num_segments=3 * m...  13.2 us
    dot_general x4, matrix products, edge_reverse_step(): jnp.dot(d_outer_b, output_weight.T, preferred_element_type=jnp.float32)  12.2 us
    gather x1, local copies, waits for them, and re-layouts, body(): sending_rows = table[table_row]  9.18 us
    gather x1, local copies, waits for them, and re-layouts, body(): grid_output_cotangent[receiver_index].reshape(blocks, block, width)  9.15 us
  transfers between devices with their start and end apart: 6, of which 2 were waited for; matrix products, arithmetic and copies ran while one was open for 13% of the time, Pallas kernels for 0%

profile of v1, /device:TPU:0, one launch (start us, length us, event | category | flops | bytes accessed | tf_op | source)
XLA Modules:
  0.0 324.8 jit_solution(12237880396287006023)
XLA Ops:
  7.2 1.3 convolution_convert_fusion
  8.5 1.3 collective-permute-start.1
  9.8 5.5 %collective-permute-start = (bf16[8,512]{1,0:T(8,128)(2,1)S(1)}, bf16[8,512]{1,0:T(8,128)(2,1)S(1)}, u32[]{:S(2)}, u32[]{:S(2)}) collective-permute-start(bf16[8,512]{1,0:T(8,128)(2,1)S(1)} %convolution_convert_fusion), channel_id=1, source_target_pairs={{0,4},{4,8},{8,12},{12,16},{16,20},{20,24},{24,28},{1,5},{5,9},{9,... | collective-permute-start | bytes 24584 | tf_op jit(solution)/shard_map/ppermute | solution.py:15
  15.3 0.7 compare_select_fusion
  16.1 0.8 compare_select_fusion.1
  16.9 1.6 fusion.27
  18.5 0.5 broadcast.290
  19.1 1.4 reduce.3
  20.5 9.2 %gather_fusion.2 = bf16[2048,512]{1,0:T(8,128)(2,1)} fusion(bf16[512,512]{1,0:T(8,128)(2,1)S(1)} %copy-done, s32[2048]{0:T(1024)S(1)} %broadcast_clamp_fusion), kind=kCustom, calls=%fused_computation.2 | custom fusion | bytes 4202496 | tf_op jit(solution)/shard_map/gather | solution.py:117
  29.6 8.9 %gather_fusion.1 = f32[2048,512]{1,0:T(8,128)} fusion(f32[512,512]{1,0:T(8,128)S(1)} %fusion.27, s32[2048]{0:T(1024)S(1)} %broadcast_clamp_fusion), kind=kCustom, calls=%fused_computation.1 | custom fusion | bytes 8396800 | tf_op jit(solution)/shard_map/gather | solution.py:116
  38.6 9.2 %gather_fusion = bf16[2048,512]{1,0:T(8,128)(2,1)} fusion(bf16[24,512]{1,0:T(8,128)(2,1)S(1)} %pad_maximum_fusion, s32[2048]{0:T(1024)S(1)} %broadcast_clamp_fusion.1), kind=kCustom, calls=%fused_computation | custom fusion | bytes 4202496 | tf_op jit(solution)/shard_map/gather | solution.py:98
  47.8 37.2 %while.16 = (s32[]{:T(128)}, f32[4,512,512]{2,1,0:T(8,128)}, f32[4,512,512]{2,1,0:T(8,128)}, f32[4,512]{1,0:T(4,128)S(1)}, f32[4,512]{1,0:T(4,128)S(1)}, /*index...) while((s32[]{:T(128)}, f32[4,512,512]{2,1,0:T(8,128)}, ...), condition=%wide.region_7.8_spmd, body=%wide.region_0.7_spmd.sunk | while | flops 816840704 | bytes 18942132 | solution.py:120
  47.8 1.7 multiply_convert_fusion.2
  49.5 1.1 constant_dynamic-slice_fusion.2
  50.8 0.5 fusion.60
  51.5 0.5 fusion.61
  52.3 1.6 fusion.63
  53.9 3.0 bitcast_dynamic-update-slice_fusion.2
  57.1 1.7 multiply_convert_fusion.2
  58.8 1.1 constant_dynamic-slice_fusion.2
  60.1 0.5 fusion.60
  61.7 1.5 fusion.63
  63.2 3.1 bitcast_dynamic-update-slice_fusion.2
  66.4 1.7 multiply_convert_fusion.2
  68.1 1.1 constant_dynamic-slice_fusion.2
  69.4 0.5 fusion.60
  71.0 1.5 fusion.63
  72.5 3.1 bitcast_dynamic-update-slice_fusion.2
  75.7 1.7 multiply_convert_fusion.2
  77.4 1.1 constant_dynamic-slice_fusion.2
  78.7 0.5 fusion.60
  79.4 0.5 fusion.61
  80.3 1.5 fusion.63
  81.7 3.0 bitcast_dynamic-update-slice_fusion.2
  84.9 13.5 %scatter_custom_fusion = f32[512,512]{1,0:T(8,128)S(1)} fusion(s32[2048]{0:T(1024)} %bitcast.107, f32[2048,512]{1,0:T(8,128)} %bitcast.108, f32[]{:T(128)} %constant.75.clone.1), kind=kCustom, calls=%fused_computation.35 | custom fusion | flops 1048576 | bytes 1049088 | tf_op jit(solution)/shard_map/scatter-add | solution.py:131
  98.4 0.9 convert_element_type.46
  99.4 13.2 %scatter_custom_fusion.1 = f32[24,512]{1,0:T(8,128)S(1)} fusion(s32[2048]{0:T(1024)S(1)} %bitcast.106, f32[2048,512]{1,0:T(8,128)} %bitcast.109, f32[]{:T(128)} %constant.75.clone.1), kind=kCustom, calls=%fused_computation.45 | custom fusion | flops 1048576 | bytes 49664 | tf_op jit(solution)/shard_map/scatter-add | solution.py:125
  112.6 4.8 %collective-permute-start.2 = (f32[8,512]{1,0:T(8,128)S(1)}, f32[8,512]{1,0:T(8,128)S(1)}, u32[]{:S(2)}, u32[]{:S(2)}) collective-permute-start(f32[8,512]{1,0:T(8,128)S(1)} %get-tuple-element.159), channel_id=1, source_target_pairs={{0,4},{4,8},{8,12},{12,16},{16,20},{20,24},{24,28},{1,5},{5,9},{9,... | collective-permute-start | bytes 49160 | tf_op jit(solution)/shard_map/ppermute | solution.py:27
  117.4 1.5 collective-permute-start.3
  118.9 3.8 %reduce_sum.81 = f32[512,512]{1,0:T(8,128)} reduce(f32[4,512,512]{2,1,0:T(8,128)} %get-tuple-element.73, f32[]{:T(128)} %constant.75.clone.1), dimensions={0}, to_apply=%region_15.16 | reduce | flops 786432 | bytes 5242884 | tf_op jit(solution)/shard_map/reduce_sum | solution.py:122
  123.1 1.3 convolution_bitcast_fusion.1
  124.4 2.3 fusion.14
  126.8 20.9 %all-reduce = (f32[512]{0:T(512)S(1)}, f32[512]{0:T(512)S(1)}) all-reduce(f32[512]{0:T(512)S(1)} %reduce_sum.82, f32[512]{0:T(512)S(1)} %reduce_sum.83), channel_id=1, replica_groups=mesh['space'=8,'level'=4] {'space'}, use_global_device_ids=true, to_apply=%region_19.20 | all-reduce | flops 1024 | bytes 8192 | tf_op jit(solution)/shard_map/psum | solution.py:144
  147.7 0.9 convolution_bitcast_fusion.2
  148.6 1.0 fusion.28
  149.6 107.6 %all-reduce.6.cloned.1.call-done = (f32[512,512]{0,1:T(8,128)}, f32[512,512]{1,0:T(8,128)}, f32[512,512]{1,0:T(8,128)}) async-done(((f32[512,512]{0,1:T(8,128)}, f32[512,512]{1,0:T(8,128)}, f32[512,512]{1,0:T(8,128)}), (f32[512,512]{0,1:T(8,128)}, f32[512,512]{1,0:T(8,128)}, f32[512,512]{1,0:T(8,128)})) %all-reduce.6.cloned.1.call-update) | async-done | bytes 3145744 | tf_op jit(solution)/shard_map/psum | solution.py:144
  257.2 59.8 %all-reduce.7 = (bf16[512,512]{0,1:T(8,128)(2,1)S(1)}, bf16[512,512]{1,0:T(8,128)(2,1)}, bf16[512,512]{1,0:T(8,128)(2,1)}, f32[512]{0:T(512)}, f32[512]{0:T(512)}) all-reduce(f32[512,512]{0,1:T(8,128)} %get-tuple-element.143, f32[512,512]{1,0:T(8,128)} %get-tuple-element.144, ...), channel_id=1, replica_groups=mesh['space'=8,'level'=4] {'level'}, use_global_device_ids=true, to_apply=%region_12.13 | all-reduce | flops 787456 | bytes 4726784 | tf_op jit(solution)/shard_map/psum | solution.py:143
  317.0 1.0 copy.21
  (79 shorter events, 5.4 us)
Async XLA Ops:
  7.2 13.3 %copy-start = (bf16[512,512]{1,0:T(8,128)(2,1)S(1)}, bf16[512,512]{1,0:T(8,128)(2,1)}, u32[]{:S(2)}) copy-start(bf16[512,512]{1,0:T(8,128)(2,1)} %param.15) | copy-start | bytes 1572868
  7.2 117.2 %reduce-scatter.2.cloned.1.call-start = ((), (), s32[]{:S(2)}) async-start(), calls=%async_computation.1 | async-start | bytes 655360 | tf_op jit(solution)/shard_map/reduce_scatter | solution.py:134
  8.5 30.0 %collective-permute-start.1 = (bf16[8,512]{1,0:T(8,128)(2,1)S(1)}, bf16[8,512]{1,0:T(8,128)(2,1)S(1)}, u32[]{:S(2)}, u32[]{:S(2)}) collective-permute-start(bf16[8,512]{1,0:T(8,128)(2,1)S(1)} %convolution_convert_fusion), channel_id=1, source_target_pairs={{4,0},{8,4},{12,8},{16,12},{20,16},{24,20},{28,24},{5,1},{9,5},{13... | collective-permute-start | bytes 24584 | tf_op jit(solution)/shard_map/ppermute | solution.py:17
  9.8 28.7 %collective-permute-start = (bf16[8,512]{1,0:T(8,128)(2,1)S(1)}, bf16[8,512]{1,0:T(8,128)(2,1)S(1)}, u32[]{:S(2)}, u32[]{:S(2)}) collective-permute-start(bf16[8,512]{1,0:T(8,128)(2,1)S(1)} %convolution_convert_fusion), channel_id=1, source_target_pairs={{0,4},{4,8},{8,12},{12,16},{16,20},{20,24},{24,28},{1,5},{5,9},{9,... | collective-permute-start | bytes 24584 | tf_op jit(solution)/shard_map/ppermute | solution.py:15
  38.5 9.2 %copy-start.1 = (bf16[512,512]{1,0:T(8,128)(2,1)S(1)}, bf16[512,512]{1,0:T(8,128)(2,1)}, u32[]{:S(2)}) copy-start(bf16[512,512]{1,0:T(8,128)(2,1)} %param.18) | copy-start | bytes 1572868
  38.5 9.2 %copy-start.5 = (f32[512]{0:T(512)S(1)}, f32[512]{0:T(512)}, u32[]{:S(2)}) copy-start(f32[512]{0:T(512)} %param.20) | copy-start | bytes 6148
  38.5 9.2 %copy-start.6 = (f32[512]{0:T(512)S(1)}, f32[512]{0:T(512)}, u32[]{:S(2)}) copy-start(f32[512]{0:T(512)} %param.19) | copy-start | bytes 6148
  84.9 38.2 %copy-start.7 = (bf16[1,8,512]{2,1,0:T(8,128)(2,1)S(1)}, bf16[1,8,512]{2,1,0:T(8,128)(2,1)}, u32[]{:S(2)}) copy-start(bf16[1,8,512]{2,1,0:T(8,128)(2,1)} %param.14) | copy-start | bytes 24580
  99.3 157.9 %all-reduce.6.cloned.1.call-start = ((), (), s32[]{:S(2)}) async-start(), calls=%async_computation.2 | async-start | bytes 6291456 | tf_op jit(solution)/shard_map/psum | solution.py:144
  112.6 10.1 %collective-permute-start.2 = (f32[8,512]{1,0:T(8,128)S(1)}, f32[8,512]{1,0:T(8,128)S(1)}, u32[]{:S(2)}, u32[]{:S(2)}) collective-permute-start(f32[8,512]{1,0:T(8,128)S(1)} %get-tuple-element.159), channel_id=1, source_target_pairs={{0,4},{4,8},{8,12},{12,16},{16,20},{20,24},{24,28},{1,5},{5,9},{9,... | collective-permute-start | bytes 49160 | tf_op jit(solution)/shard_map/ppermute | solution.py:27
  117.4 5.6 %collective-permute-start.3 = (f32[8,512]{1,0:T(8,128)S(1)}, f32[8,512]{1,0:T(8,128)S(1)}, u32[]{:S(2)}, u32[]{:S(2)}) collective-permute-start(f32[8,512]{1,0:T(8,128)S(1)} %get-tuple-element.160), channel_id=1, source_target_pairs={{4,0},{8,4},{12,8},{16,12},{20,16},{24,20},{28,24},{5,1},{9,5},{13... | collective-permute-start | bytes 49160 | tf_op jit(solution)/shard_map/ppermute | solution.py:27
  118.9 28.8 %copy-start.2 = (bf16[512,512]{1,0:T(8,128)(2,1)S(1)}, bf16[512,512]{1,0:T(8,128)(2,1)}, u32[]{:S(2)}) copy-start(bf16[512,512]{1,0:T(8,128)(2,1)} %param.16) | copy-start | bytes 1572868
  122.8 25.8 %copy-start.3 = (bf16[512,512]{1,0:T(8,128)(2,1)S(1)}, bf16[512,512]{1,0:T(8,128)(2,1)}, u32[]{:S(2)}) copy-start(bf16[512,512]{1,0:T(8,128)(2,1)} %param.17) | copy-start | bytes 1572868
  124.4 24.1 %copy-start.4 = (bf16[128,512]{1,0:T(8,128)(2,1)S(1)}, bf16[128,512]{1,0:T(8,128)(2,1)}, u32[]{:S(2)}) copy-start(bf16[128,512]{1,0:T(8,128)(2,1)} %reduce-scatter.2.cloned.1.call-done) | copy-start | bytes 393220
Sparse Core Ops, SparseCore 0:
  99.4 23.2 reduce-scatter.1
  126.9 130.2 all-reduce.5
